TPU v7x, 256 devices: a whole 4x4x8 slice. The times are simulated.
256 devices in a mesh: dp: 16 (over z, x_lo), tensor: 16 (over x_hi, y, core).
Axes of the slice: x: 4 (x_hi: 2, x_lo: 2; x = x_hi * 2 + x_lo), y: 4, z: 8, core: 2. Of those that a mesh axis runs over, the one named last changes fastest.
Arguments:
- hidden_in: bfloat16 [256, 128, 4096], P(('dp', 'tensor')), parts along dimension 0, may hold values from -6 to 6
- norm_gain: float32 [4096], replicated, may hold values from 0.1 to 1.9
- query_weight: bfloat16 [4096, 4096], P(None, 'tensor'), may hold values from -3 to 3
- kv_weight: bfloat16 [4096, 2048], P(None, 'tensor'), may hold values from -3 to 3
- output_weight: bfloat16 [4096, 4096], P('tensor'), may hold values from -0.09375 to 0.09375
Outputs:
- attention_out: bfloat16 [256, 128, 4096], P(('dp', 'tensor')), parts along dimension 0
There are 16 independent parts, one for each index of `dp`. A program takes and returns all parts, laid end to end along the dimension named above; an argument that names none is the same for every part. Nothing has to cross between parts.
All inputs are finite; a program needn't handle non-finite values.
Results may differ from a plain program's by a relative error of at most 0.014.
The roundings to bfloat16 on the way count: a program that leaves them out, or rounds other values in their place, can miss the bound.
Values may be sent and summed in bfloat16 or wider, within the bound.
A program may use at most 128 MiB of HBM per device.

v0:
```python
import math

import jax
import jax.numpy as jnp
from jax import lax
from jax.sharding import PartitionSpec as P

HD = 128


EPS = 1e-05
THETA = 500000.0


def partner_2(value, axis, bit):
    mask = 2**bit
    pairs = [(source, source ^ mask) for source in range(lax.axis_size(axis))]
    return lax.ppermute(value, axis, pairs)


def rotary(tensor, positions):
    half_width = tensor.shape[-1] // 2
    frequency = THETA ** (-(jnp.arange(half_width, dtype=jnp.float32) * 2.0 / tensor.shape[-1]))
    angles = positions[:, None] * frequency[None, :]
    cosine = jnp.cos(angles)[:, None, :]
    sine_part = jnp.sin(angles)[:, None, :]
    first_half = tensor[..., :half_width]
    second_half = tensor[..., half_width:]
    return jnp.concatenate(
        (
            first_half * cosine - second_half * sine_part,
            second_half * cosine + first_half * sine_part,
        ),
        axis=-1,
    )


def rms_norm(hidden_in, norm_gain):
    wide = hidden_in.astype(jnp.float32)
    mean_square = jnp.mean(wide * wide, axis=-1, keepdims=True)
    return (wide * lax.rsqrt(mean_square + EPS) * norm_gain).astype(jnp.bfloat16)


def attend(queries, keys, values):
    length = queries.shape[1]
    scores = jnp.einsum(
        "bqhgd,bkhd->bhgqk", queries, keys, preferred_element_type=jnp.float32
    ) / math.sqrt(queries.shape[-1])
    causal = jnp.arange(length)[:, None] >= jnp.arange(length)[None, :]
    scores = jnp.where(causal, scores, -1e30)
    highest = jnp.max(scores, axis=-1, keepdims=True)
    exponent = jnp.exp(scores - highest)
    probabilities = (exponent / jnp.sum(exponent, axis=-1, keepdims=True)).astype(jnp.bfloat16)
    mixed = jnp.einsum(
        "bhgqk,bkhd->bqhgd", probabilities, values, preferred_element_type=jnp.float32
    )
    return mixed.astype(jnp.bfloat16)


def join_heads(stacked, axis_dim):
    position = lax.axis_index("tensor")
    partner = partner_2(stacked, "tensor", 0)
    keeps_first = position // (1 << 0) % 2 == 0
    stacked = jnp.where(
        keeps_first,
        jnp.concatenate((stacked, partner), axis_dim),
        jnp.concatenate((partner, stacked), axis_dim),
    )
    return stacked


def shards(hidden_in, norm_gain, query_weight, kv_weight, output_weight):
    merged_weight = jnp.concatenate((query_weight, kv_weight), axis=1)
    query_cols = query_weight.shape[1]
    normed = rms_norm(hidden_in, norm_gain)
    projected = jnp.einsum(
        "brd,dc->brc",
        lax.all_gather(normed, "tensor", axis=0, tiled=True),
        merged_weight,
        preferred_element_type=jnp.float32,
    )
    batch, length = (projected.shape[0], projected.shape[1])
    queries_raw = projected[..., :query_cols]
    kv_raw = projected[..., query_cols:].astype(jnp.bfloat16)
    kv_raw = join_heads(kv_raw, 2)
    kv_heads = kv_raw.shape[-1] // (2 * HD)
    kv_split = kv_raw.reshape(batch, length, kv_heads, 2, HD)
    keys_raw = kv_split[:, :, :, 0, :]
    values = kv_split[:, :, :, 1, :]
    heads = query_cols // HD
    positions = jnp.arange(length, dtype=jnp.float32)
    queries = rotary(queries_raw.reshape(batch, length, heads, HD), positions).astype(jnp.bfloat16)
    keys = rotary(keys_raw.astype(jnp.float32), positions).astype(jnp.bfloat16)
    mixed = attend(queries.reshape(batch, length, kv_heads, heads // kv_heads, HD), keys, values)
    mixed_rows = mixed.reshape(batch, length, heads * HD)
    partial_out = jnp.einsum(
        "blc,cd->bld", mixed_rows, output_weight, preferred_element_type=jnp.float32
    )
    return lax.psum_scatter(
        partial_out.astype(jnp.bfloat16), "tensor", scatter_dimension=0, tiled=True
    )


def solution(mesh):
    placed = (
        P(("dp", "tensor"), None, None),
        P(),
        P(None, "tensor"),
        P(None, "tensor"),
        P("tensor", None),
    )
    return jax.shard_map(
        shards,
        mesh=mesh,
        in_specs=placed,
        out_specs=P(("dp", "tensor"), None, None),
        check_vma=False,
    )
```

profile of v0, /device:TPU:1, one launch (start us, length us, event | category | flops | bytes accessed | tf_op | source)
XLA Modules:
  0.0 333.6 jit_solution(4753455805095403409)
XLA Ops:
  6.5 0.0 copy-start
  6.5 0.0 all-gather.2.cloned.1.call-start
  6.5 1.7 fusion.3
  8.2 2.5 fusion.5
  10.8 0.0 all-gather.2.cloned.1.call-update
  10.8 0.0 reduce-scatter.2.cloned.1.call-start
  10.9 0.3 fusion.19
  11.1 117.7 %all-gather.2.cloned.1.call-done = bf16[16,128,4096]{2,1,0:T(8,128)(2,1)} async-done(((bf16[1,128,4096]{2,1,0:T(8,128)(2,1)}), bf16[16,128,4096]{2,1,0:T(8,128)(2,1)}) %all-gather.2.cloned.1.call-update) | async-done | bytes 16777232 | tf_op jit(solution)/shard_map/all_gather | solution.py:78
  128.8 0.0 copy-done.3
  128.8 12.2 %fusion = f32[16,128,384]{2,1,0:T(8,128)S(1)} fusion(bf16[16,128,4096]{2,1,0:T(8,128)(2,1)} %all-gather.2.cloned.1.call-done, bf16[4096,128]{1,0:T(8,128)(2,1)S(1)} %copy-done.3, bf16[4096,256]{1,0:T(8,128)(2,1)} %param.7), kind=kOutput, calls=%fused_computation.2 | convolution fusion | flops 6448742400 | bytes 23068672 | tf_op jit(solution)/shard_map/brd,dc->brc/dot_general | solution.py:76
  141.1 1.5 slice.38
  142.6 0.1 slice.54
  142.7 3.3 reshape.137
  146.0 0.3 collective-permute-start
  146.2 4.5 %fusion.22 = (f32[16,128,2,64]{3,2,1,0:T(2,128)S(1)}, f32[16,128,2,64]{3,2,1,0:T(2,128)S(1)}) fusion(f32[16,128,2,128]{3,2,1,0:T(2,128)} %reshape.137), kind=kLoop, calls=%fused_computation.42 | loop fusion | bytes 4194304 | tf_op jit(solution)/shard_map/slice | solution.py:27
  150.8 2.0 subtract_convert_fusion
  152.8 0.0 collective-permute-done
  152.8 1.4 maximum_select_fusion
  154.2 1.3 select_n.34
  155.5 2.3 fusion.23
  157.8 0.1 fusion.16
  157.9 0.0 copy-start.1
  157.9 1.5 fusion.12
  159.4 3.5 %copy.22 = bf16[16,128,1,1,128]{1,4,0,3,2:T(8,128)(2,1)} copy(bf16[16,128,1,1,128]{4,3,1,0,2:T(2,128)(2,1)} %get-tuple-element.11) | data formatting | bytes 1048576
  162.9 0.0 copy-done.1
  162.9 2.7 fusion.24
  165.5 0.4 fusion.7
  165.9 0.7 copy-done.2
  166.6 0.6 convolution_convert_fusion.1
  167.2 8.1 %convolution_convert_fusion = bf16[16,128,4096]{2,1,0:T(8,128)(2,1)} fusion(bf16[16,128,256]{1,2,0:T(8,128)(2,1)S(1)} %bitcast.43, bf16[256,4096]{1,0:T(8,128)(2,1)S(1)} %copy-done), kind=kOutput, calls=%fused_computation | convolution fusion | flops 4303355904 | bytes 19922944 | tf_op jit(solution)/shard_map/blc,cd->bld/dot_general | solution.py:96
  175.2 0.0 reduce-scatter.2.cloned.1.call-update
  175.3 151.5 %reduce-scatter.2.cloned.1.call-done = bf16[1,128,4096]{2,1,0:T(8,128)(2,1)} async-done(((bf16[16,128,4096]{2,1,0:T(8,128)(2,1)}), bf16[1,128,4096]{2,1,0:T(8,128)(2,1)}) %reduce-scatter.2.cloned.1.call-update) | async-done | bytes 1048592 | tf_op jit(solution)/shard_map/reduce_scatter | solution.py:99
  (6 shorter events, 0.0 us)
Async XLA Ops:
  6.5 160.6 %copy-start = (bf16[256,4096]{1,0:T(8,128)(2,1)S(1)}, bf16[256,4096]{1,0:T(8,128)(2,1)}, u32[]{:S(2)}) copy-start(bf16[256,4096]{1,0:T(8,128)(2,1)} %param.9) | copy-start | bytes 6291460
  6.5 122.3 %copy-start.3 = (bf16[4096,128]{1,0:T(8,128)(2,1)S(1)}, bf16[4096,128]{1,0:T(8,128)(2,1)}, u32[]{:S(2)}) copy-start(bf16[4096,128]{1,0:T(8,128)(2,1)} %param.8) | copy-start | bytes 3145732
  6.5 122.3 %all-gather.2.cloned.1.call-start = ((), (), s32[]{:S(2)}) async-start(), calls=%async_computation.1 | async-start | bytes 17825792 | tf_op jit(solution)/shard_map/all_gather | solution.py:78
  10.8 316.0 %reduce-scatter.2.cloned.1.call-start = ((), (), s32[]{:S(2)}) async-start(), calls=%async_computation.2 | async-start | bytes 17825792 | tf_op jit(solution)/shard_map/reduce_scatter | solution.py:99
  146.0 6.8 %collective-permute-start = (bf16[16,128,128]{2,1,0:T(8,128)(2,1)S(1)}, bf16[16,128,128]{2,1,0:T(8,128)(2,1)S(1)}, u32[]{:S(2)}, u32[]{:S(2)}) collective-permute-start(bf16[16,128,128]{2,1,0:T(8,128)(2,1)S(1)} %slice.54), channel_id=1, source_target_pairs={{0,1},{1,0},{2,3},{3,2},{4,5},{5,4},{6,7},{7,6},{8,9},{9,8},{10,11... | collective-permute-start | bytes 1572872 | tf_op jit(solution)/shard_map/ppermute | solution.py:18
  157.9 4.9 %copy-start.1 = (bf16[16,128,2,64]{3,1,2,0:T(8,128)(2,1)S(1)}, bf16[16,128,2,64]{3,1,2,0:T(8,128)(2,1)}, u32[]{:S(2)}) copy-start(bf16[16,128,2,64]{3,1,2,0:T(8,128)(2,1)} %get-tuple-element.5) | copy-start | bytes 1572868
  165.5 1.0 copy-start.2
Sparse Core Ops, SparseCore 0:
  10.9 117.9 all-gather.1
  175.4 151.2 reduce-scatter.1
where the time goes:
time: 334 us
  waiting for transfers between devices  269 us (81%)
  matrix products  23.6 us (7%)
  local copies, waits for them, and re-layouts  17.2 us (5%)
  between operations  13.5 us (4%)
  other arithmetic  9.81 us (3%)
    reduce_scatter x1, waiting for transfers between devices, shards(): lax.psum_scatter(partial_out.astype(jnp.bfloat16), 'tensor', scatter_dime...  151 us
    all_gather x1, waiting for transfers between devices, shards(): lax.all_gather(normed, 'tensor', axis=0, tiled=True)  118 us
    dot_general x1, matrix products, shards(): jnp.einsum('brd,dc->brc', lax.all_gather(normed, 'tensor', axis=0, tiled=...  12.2 us
    dot_general x1, matrix products, shards(): jnp.einsum('blc,cd->bld', mixed_rows, output_weight, preferred_element_ty...  8.09 us
  transfers between devices with their start and end apart: 3, of which 2 were waited for; matrix products, arithmetic and copies ran while one was open for 2% of the time, Pallas kernels for 0%

commit v1 on v0

v1 whole, which is shorter than its diff:
```python
import math

import jax
import jax.numpy as jnp
import numpy as np
from jax import lax
from jax.experimental import pallas as pl
from jax.experimental.pallas import tpu as pltpu
from jax.sharding import PartitionSpec as P

HD = 128
EPS = 1e-05
THETA = 500000.0
SEQ = 128
D = 4096
HALF = SEQ // 2
RC = 16
NCH = HALF // RC
NS = 4
STEPS = 2 * NS
BF = jnp.bfloat16
F32 = jnp.float32
MESH = pl.DeviceIdType.MESH


def tables():
    i = np.arange(HD // 2, dtype=np.float64)
    ang = np.arange(SEQ, dtype=np.float64)[:, None] * THETA ** (-2.0 * i / HD)[None, :]
    cos, sin = np.cos(ang), np.sin(ang)
    return np.stack(
        [np.concatenate([cos, cos], 1), np.concatenate([-sin, sin], 1)]
    ).astype(np.float32)


def kernel(
    h, gain, tab, wq, wkv, wo, out,
    hbuf, xn, gain_v, tab_v, wq_v, wkv_v, wo_v, mx,
    acc, comb, sbuf, rd, rf, ob,
    sem_l, sem_o, ag_s, ag_r, w_s, w_r, po_s, po_r, rs_s, rs_r,
):
    dp = lax.axis_index("dp")
    t = lax.axis_index("tensor")
    z, xl = dp // 2, dp % 2
    xh, y, c = t // 8, (t // 2) % 4, t % 2
    b = z % 2

    def at_y(yy):
        return (dp, xh * 8 + yy * 2 + c)

    right, left = at_y((y + 1) % 4), at_y((y + 3) % 4)
    cross = (z * 2 + 1 - xl, (1 - xh) * 8 + y * 2 + c)
    xlo = (z * 2 + 1 - xl, t)
    zp = (((z + 1) % 8) * 2 + xl, t)
    zm = (((z + 7) % 8) * 2 + xl, t)
    part = (dp, t + 1 - 2 * c)

    def remote(src, dst, ss, rs, dev):
        return pltpu.make_async_remote_copy(
            src_ref=src, dst_ref=dst, send_sem=ss, recv_sem=rs,
            device_id=dev, device_id_type=MESH,
        )

    loads = [
        pltpu.make_async_copy(h.at[0], hbuf.at[0], sem_l.at[0]),
        pltpu.make_async_copy(gain, gain_v, sem_l.at[1]),
        pltpu.make_async_copy(tab, tab_v, sem_l.at[2]),
        pltpu.make_async_copy(wq, wq_v.at[0, c], sem_l.at[3]),
        pltpu.make_async_copy(
            wkv, wkv_v.at[0, :, pl.ds(pl.multiple_of(c * HD, HD), HD)], sem_l.at[4]
        ),
        pltpu.make_async_copy(wo, wo_v.at[0, c], sem_l.at[5]),
    ]
    for cp in loads:
        cp.start()

    barrier = pltpu.get_barrier_semaphore()
    for dev in (right, left, cross, xlo, zp, zm, part):
        pl.semaphore_signal(barrier, inc=1, device_id=dev, device_id_type=MESH)
    pl.semaphore_wait(barrier, 7)

    sent = []

    def go(cp):
        cp.start()
        sent.append(cp)

    def rows(ref, half):
        return ref.at[pl.ds(half * HALF, HALF), :]

    def ag_own(direction, half):
        dst = hbuf.at[1 if direction == 0 else 2]
        return remote(
            rows(h.at[0], half), rows(dst, half),
            ag_s.at[direction, half], ag_r.at[1 + direction, half],
            right if direction == 0 else left,
        )

    def ag_fwd(direction):
        half = direction
        return remote(
            rows(hbuf.at[1 + direction], half), rows(hbuf.at[3], half),
            ag_s.at[direction, 2], ag_r.at[3, half],
            right if direction == 0 else left,
        )

    def ag_wait(slot, half):
        remote(
            rows(hbuf.at[slot], half), rows(hbuf.at[slot], half),
            ag_s.at[0, 0], ag_r.at[slot, half], right,
        ).wait_recv()

    go(ag_own(0, 0))
    go(ag_own(1, 1))
    go(ag_own(0, 1))
    go(ag_own(1, 0))

    def region(m, g, core, q, i):
        if m == 0:
            return wq_v.at[g, core, pl.ds(q * 1024 + i * 256, 256), :]
        if m == 1:
            return wkv_v.at[
                g, pl.ds(q * 1024 + i * 256, 256),
                pl.ds(pl.multiple_of(core * HD, HD), HD),
            ]
        return wo_v.at[g, core, pl.ds(q * 64 + i * 16, 16), :]

    def own_region(m, q, i):
        if m == 0:
            return wq.at[pl.ds(q * 1024 + i * 256, 256), :]
        if m == 1:
            return wkv.at[pl.ds(q * 1024 + i * 256, 256), :]
        return wo.at[pl.ds(q * 64 + i * 16, 16), :]

    def parts(s):
        return [(0, s), (1, s)] if s < NS else [(2, s - NS)]

    def sem_ix(m, i):
        return m * NS + i

    q_cc = 2 * xl + b
    q_x = 2 * (1 - xl) + b
    q_zc = 2 * xl + 1 - b
    q_zx = 2 * (1 - xl) + 1 - b

    def cross_send(s):
        for m, i in parts(s):
            q = 2 * (1 - xl) + b
            k = sem_ix(m, i)
            go(remote(own_region(m, q, i), region(m, 1, c, q, i),
                      w_s.at[0, k], w_r.at[0, k], cross))

    def w_wait(ch, m, core, q, i):
        k = sem_ix(m, i)
        reg = region(m, 1, core, q, i)
        remote(reg, reg, w_s.at[ch, k], w_r.at[ch, k], part).wait_recv()

    def w_send(ch, m, q, i, dev):
        k = sem_ix(m, i)
        reg = region(m, 1, c, q, i)
        go(remote(reg, reg, w_s.at[ch, k], w_r.at[ch, k], dev))

    def z_dev(i):
        return zp if i % 2 == 0 else zm

    def relay(T):
        if 0 <= T < STEPS:
            for m, i in parts(T):
                w_wait(0, m, c, q_cc, i)
                w_send(1, m, q_cc, i, xlo)
                w_send(2, m, q_cc, i, z_dev(i))
                w_send(4, m, q_cc, i, part)
        if 0 <= T - 1 < STEPS:
            for m, i in parts(T - 1):
                w_wait(1, m, c, q_x, i)
                w_send(3, m, q_x, i, z_dev(i))
                w_send(5, m, q_x, i, part)
            for m, i in parts(T - 1):
                w_wait(2, m, c, q_zc, i)
                w_send(6, m, q_zc, i, part)
        if 0 <= T - 2 < STEPS:
            for m, i in parts(T - 2):
                w_wait(3, m, c, q_zx, i)
                w_send(7, m, q_zx, i, part)

    def part_wait(m):
        for i in range(NS):
            for ch, q in ((4, q_cc), (5, q_x), (6, q_zc), (7, q_zx)):
                w_wait(ch, m, 1 - c, q, i)

    def own_to_part(m):
        src = (wq, wkv, wo)[m]
        dst = (
            wq_v.at[0, c],
            wkv_v.at[0, :, pl.ds(pl.multiple_of(c * HD, HD), HD)],
            wo_v.at[0, c],
        )[m]
        return remote(src, dst, po_s.at[m], po_r.at[m], part)

    def own_part_wait(m):
        dst = (
            wq_v.at[0, 1 - c],
            wkv_v.at[0, :, pl.ds(pl.multiple_of((1 - c) * HD, HD), HD)],
            wo_v.at[0, 1 - c],
        )[m]
        remote(dst, dst, po_s.at[m], po_r.at[m], part).wait_recv()

    for s in range(STEPS):
        cross_send(s)
    for m in range(3):
        go(own_to_part(m))

    def norm(slot):
        @pl.loop(0, SEQ // 16)
        def _(r):
            r0 = pl.multiple_of(r * 16, 16)
            wide = hbuf[slot, pl.ds(r0, 16), :].astype(F32)
            ms = jnp.mean(wide * wide, axis=-1, keepdims=True)
            xn[slot, pl.ds(r0, 16), :] = (
                wide * lax.rsqrt(ms + EPS) * gain_v[...]
            ).astype(BF)

    def rope(v):
        return v * tab_v[0] + pltpu.roll(v, HD // 2, 1) * tab_v[1]

    def attn(slot, g):
        x = xn[slot]
        kv = jnp.dot(x, wkv_v[g], preferred_element_type=F32).astype(BF)
        q0 = jnp.dot(x, wq_v[g, 0], preferred_element_type=F32)
        q1 = jnp.dot(x, wq_v[g, 1], preferred_element_type=F32)
        keys = rope(kv[:, :HD].astype(F32)).astype(BF)
        vals = kv[:, HD:]
        qs = jnp.concatenate(
            [rope(v).astype(BF) for v in (q0[:, :HD], q0[:, HD:], q1[:, :HD], q1[:, HD:])],
            axis=0,
        )
        sc = lax.dot_general(
            qs, keys, (((1,), (1,)), ((), ())), preferred_element_type=F32
        ) * (1.0 / math.sqrt(HD))
        rowi = lax.broadcasted_iota(jnp.int32, sc.shape, 0) % SEQ
        coli = lax.broadcasted_iota(jnp.int32, sc.shape, 1)
        sc = jnp.where(rowi >= coli, sc, -1e30)
        e = jnp.exp(sc - jnp.max(sc, axis=-1, keepdims=True))
        p = (e / jnp.sum(e, axis=-1, keepdims=True)).astype(BF)
        o = jnp.dot(p, vals, preferred_element_type=F32).astype(BF)
        for j in range(4):
            mx[slot, :, pl.ds(g * 512 + j * HD, HD)] = o[j * SEQ:(j + 1) * SEQ]

    NB = 512

    def outp(slot):
        @pl.loop(0, D // NB)
        def _(n):
            cols = pl.ds(pl.multiple_of(n * NB, NB), NB)
            o = jnp.zeros((SEQ, NB), F32)
            for k in range(4):
                o = o + jnp.dot(
                    mx[slot, :, pl.ds(k * 256, 256)], wo_v[k // 2, k % 2, :, cols],
                    preferred_element_type=F32,
                )
            if slot == 0:
                acc[:, cols] = o
            elif slot == 1:
                sbuf[0, pl.ds(0, HALF), cols] = o[:HALF].astype(BF)
                comb[1, :, cols] = o[HALF:]
            elif slot == 2:
                sbuf[1, pl.ds(HALF, HALF), cols] = o[HALF:].astype(BF)
                comb[0, :, cols] = o[:HALF]
            else:
                sbuf[2, :, cols] = o.astype(BF)

    def rc(ref, half, r):
        return ref.at[pl.ds(half * HALF + r * RC, RC), :]

    def rs_only(direction):
        half = 1 - direction
        src = sbuf.at[1 - direction]
        return remote(rows(src, half), rows(rf.at[direction], half),
                      rs_s.at[direction, 0], rs_r.at[direction, 0],
                      right if direction == 0 else left)

    def rs_diag(direction, r):
        return remote(rc(sbuf.at[2], direction, r),
                      rd.at[direction, pl.ds(r * RC, RC), :],
                      rs_s.at[direction, 1 + r], rs_r.at[direction, 1 + r],
                      right if direction == 0 else left)

    def rs_comb(direction, r):
        k = 1 + NCH + r
        return remote(rc(sbuf.at[1 - direction], direction, r),
                      rc(rf.at[direction], direction, r),
                      rs_s.at[direction, k], rs_r.at[direction, k],
                      right if direction == 0 else left)

    loads[0].wait()
    loads[1].wait()
    norm(0)
    relay(0)
    relay(1)
    for cp in loads[2:5]:
        cp.wait()
    own_part_wait(0)
    own_part_wait(1)
    attn(0, 0)
    ag_wait(1, 0)
    ag_wait(2, 1)
    go(ag_fwd(0))
    go(ag_fwd(1))
    relay(2)
    relay(3)
    relay(4)
    ag_wait(1, 1)
    norm(1)
    ag_wait(2, 0)
    norm(2)
    attn(1, 0)
    relay(5)
    attn(2, 0)
    part_wait(0)
    part_wait(1)
    attn(0, 1)
    relay(6)
    attn(1, 1)
    relay(7)
    attn(2, 1)
    relay(8)
    ag_wait(3, 0)
    ag_wait(3, 1)
    norm(3)
    attn(3, 0)
    relay(9)
    loads[5].wait()
    own_part_wait(2)
    part_wait(2)
    outp(2)
    go(rs_only(0))
    outp(1)
    go(rs_only(1))
    attn(3, 1)
    outp(3)
    for r in range(NCH):
        go(rs_diag(0, r))
        go(rs_diag(1, r))
    outp(0)
    for r in range(NCH):
        for direction in (0, 1):
            rs_diag(direction, r).wait_recv()
            rr = pl.ds(r * RC, RC)
            v = comb[direction, rr, :] + rd[direction, rr, :].astype(F32)
            sbuf[1 - direction, pl.ds(direction * HALF + r * RC, RC), :] = v.astype(BF)
            go(rs_comb(direction, r))
    rs_only(0).wait_recv()
    rs_only(1).wait_recv()
    outs = []
    for r in range(NCH):
        for half in (0, 1):
            rs_comb(half, r).wait_recv()
            rr = pl.ds(half * HALF + r * RC, RC)
            v = acc[rr, :] + rf[0, rr, :].astype(F32) + rf[1, rr, :].astype(F32)
            ob[rr, :] = v.astype(BF)
            cp = pltpu.make_async_copy(
                ob.at[rr, :], out.at[0, rr, :], sem_o.at[half, r]
            )
            cp.start()
            outs.append(cp)
    for cp in outs:
        cp.wait()
    for cp in sent:
        cp.wait_send()


def shards(hidden_in, norm_gain, query_weight, kv_weight, output_weight):
    tab = jnp.asarray(tables())
    anyspec = pl.BlockSpec(memory_space=pl.ANY)
    dma = pltpu.SemaphoreType.DMA
    return pl.pallas_call(
        kernel,
        out_shape=jax.ShapeDtypeStruct((1, SEQ, D), BF),
        in_specs=[anyspec] * 6,
        out_specs=anyspec,
        scratch_shapes=[
            pltpu.VMEM((4, SEQ, D), BF),
            pltpu.VMEM((4, SEQ, D), BF),
            pltpu.VMEM((1, D), F32),
            pltpu.VMEM((2, SEQ, HD), F32),
            pltpu.VMEM((2, 2, D, 2 * HD), BF),
            pltpu.VMEM((2, D, 2 * HD), BF),
            pltpu.VMEM((2, 2, 2 * HD, D), BF),
            pltpu.VMEM((4, SEQ, 1024), BF),
            pltpu.VMEM((SEQ, D), F32),
            pltpu.VMEM((2, HALF, D), F32),
            pltpu.VMEM((3, SEQ, D), BF),
            pltpu.VMEM((2, HALF, D), BF),
            pltpu.VMEM((2, SEQ, D), BF),
            pltpu.VMEM((SEQ, D), BF),
            dma((6,)),
            dma((2, NCH)),
            dma((2, 3)),
            dma((4, 2)),
            dma((8, 3 * NS)),
            dma((8, 3 * NS)),
            dma((3,)),
            dma((3,)),
            dma((2, 1 + 2 * NCH)),
            dma((2, 1 + 2 * NCH)),
        ],
        compiler_params=pltpu.CompilerParams(
            collective_id=0, has_side_effects=True, vmem_limit_bytes=67000000
        ),
        cost_estimate=pl.CostEstimate(
            flops=11_000_000_000, bytes_accessed=8_000_000, transcendentals=600_000
        ),
    )(hidden_in, norm_gain.reshape(1, D), tab, query_weight, kv_weight, output_weight)


def solution(mesh):
    placed = (
        P(("dp", "tensor"), None, None),
        P(),
        P(None, "tensor"),
        P(None, "tensor"),
        P("tensor", None),
    )
    return jax.shard_map(
        shards,
        mesh=mesh,
        in_specs=placed,
        out_specs=P(("dp", "tensor"), None, None),
        check_vma=False,
    )
```

time: 334 us -> 102 us (0.31)
  waiting for transfers between devices: 269 us -> 0 us
  Pallas kernels: 0 us -> 99.6 us
  matrix products: 23.6 us -> 0 us
  local copies, waits for them, and re-layouts: 17.2 us -> 2.29 us
  between operations: 13.5 us -> 0.01 us
  other arithmetic: 9.81 us -> 0 us
    reduce_scatter x1 -> x0, waiting for transfers between devices: 151 us -> none  [shards(): lax.psum_scatter(partial_out.astype(jnp.bfloat16), 'tensor', scatter_dime...]
    all_gather x1 -> x0, waiting for transfers between devices: 118 us -> none  [shards(): lax.all_gather(normed, 'tensor', axis=0, tiled=True)]
    pallas_call x0 -> x1, Pallas kernels: none -> 99.6 us  [shards(): pl.pallas_call(kernel, out_shape=jax.ShapeDtypeStruct((1, SEQ, D), BF), i...]
    dot_general x4 -> x0, matrix products: 23.6 us -> none  [the longest x1 12.2 us: shards(): jnp.einsum('brd,dc->brc', lax.all_gather(normed, 'tensor', axis=0, tiled=...]
    slice x4 -> x0, local copies, waits for them, and re-layouts: 8.45 us -> none  [the longest x1 4.55 us: rotary(): first_half = tensor[..., :half_width]]
  transfers between devices with their start and end apart: 3 -> 0, of which waited for: 2 -> 0; matrix products, arithmetic and copies ran while one was open for 2% -> 0% of each run, Pallas kernels for 0% -> 0%
where the time goes in v1:
time: 102 us
  Pallas kernels  99.6 us (98%)
  local copies, waits for them, and re-layouts  2.29 us (2%)
    pallas_call x1, Pallas kernels, shards(): pl.pallas_call(kernel, out_shape=jax.ShapeDtypeStruct((1, SEQ, D), BF), i...  99.6 us
    unnamed x1, local copies, waits for them, and re-layouts  2.29 us

profile of v1, /device:TPU:1, one launch (start us, length us, event | category | flops | bytes accessed | tf_op | source)
XLA Modules:
  0.0 101.9 jit_solution(3188302328168732088)
XLA Ops:
  0.0 99.6 %shard_map.64 = bf16[1,128,4096]{2,1,0:T(8,128)(2,1)} custom-call(bf16[1,128,4096]{2,1,0:T(8,128)(2,1)} %h.1, f32[1,4096]{1,0:T(1,128)} %bitcast.1, f32[2,128,128]{2,1,0:T(8,128)} %constant.2.clone.tab, bf16[4096,256]{1,0:T(8,128)(2,1)} %wq.1, bf16[4096,128]{1,0:T(8,128)(2,1)} %wkv.1, bf16[256,4096]{1,0:T(8,128)(2,1)} %wo.1), custom_call_target="tpu_custom_call" | custom-call | flops 11000000512 | bytes 8000000 | tf_op jit(solution)/shard_map/pallas_call | solution.py:375
  99.6 2.3 %copy.8 = bf16[1,128,4096]{2,1,0:T(8,128)(2,1)} copy(bf16[1,128,4096]{2,1,0:T(8,128)(2,1)} %shard_map.64) | data formatting | bytes 2097152

commit v2 on v1

v2 whole, which is shorter than its diff:
```python
import math

import jax
import jax.numpy as jnp
import numpy as np
from jax import lax
from jax.experimental import pallas as pl
from jax.experimental.pallas import tpu as pltpu
from jax.sharding import PartitionSpec as P

HD = 128
EPS = 1e-05
THETA = 500000.0
SEQ = 128
D = 4096
HALF = SEQ // 2
CW = 1024
NC = D // CW
NQ = 8
NSTEP = NQ + NC
BF = jnp.bfloat16
F32 = jnp.float32
MESH = pl.DeviceIdType.MESH


def tables():
    i = np.arange(HD // 2, dtype=np.float64)
    ang = np.arange(SEQ, dtype=np.float64)[:, None] * THETA ** (-2.0 * i / HD)[None, :]
    cos, sin = np.cos(ang), np.sin(ang)
    return np.stack(
        [np.concatenate([cos, cos], 1), np.concatenate([-sin, sin], 1)]
    ).astype(np.float32)


def kernel(
    h, gain, tab, wq, wkv, wo, out,
    hbuf, xn, gain_v, tab_v, wq_v, wkv_v, wo_v, mx,
    acc, comb, sbuf, rd, rf, ob,
    sem_l, sem_o, ag_s, ag_r, w_s, w_r, po_s, po_r, rs_s, rs_r,
):
    dp = lax.axis_index("dp")
    t = lax.axis_index("tensor")
    z, xl = dp // 2, dp % 2
    xh, y, c = t // 8, (t // 2) % 4, t % 2
    b = z % 2

    def at_y(yy):
        return (dp, xh * 8 + yy * 2 + c)

    right, left = at_y((y + 1) % 4), at_y((y + 3) % 4)
    cross = (z * 2 + 1 - xl, (1 - xh) * 8 + y * 2 + c)
    xlo = (z * 2 + 1 - xl, t)
    zp = (((z + 1) % 8) * 2 + xl, t)
    zm = (((z + 7) % 8) * 2 + xl, t)
    part = (dp, t + 1 - 2 * c)

    def remote(src, dst, ss, rs, dev):
        return pltpu.make_async_remote_copy(
            src_ref=src, dst_ref=dst, send_sem=ss, recv_sem=rs,
            device_id=dev, device_id_type=MESH,
        )

    loads = [
        pltpu.make_async_copy(h.at[0], hbuf.at[0], sem_l.at[0]),
        pltpu.make_async_copy(gain, gain_v, sem_l.at[1]),
        pltpu.make_async_copy(tab, tab_v, sem_l.at[2]),
        pltpu.make_async_copy(wq, wq_v.at[0, c], sem_l.at[3]),
        pltpu.make_async_copy(
            wkv, wkv_v.at[0, :, pl.ds(pl.multiple_of(c * HD, HD), HD)], sem_l.at[4]
        ),
        pltpu.make_async_copy(
            wo, wo_v.at[pl.ds(pl.multiple_of(c * 256, 256), 256), :], sem_l.at[5]
        ),
    ]
    for cp in loads:
        cp.start()

    barrier = pltpu.get_barrier_semaphore()
    for dev in (right, left, cross, xlo, zp, zm, part):
        pl.semaphore_signal(barrier, inc=1, device_id=dev, device_id_type=MESH)
    pl.semaphore_wait(barrier, 7)

    sent = []

    def go(cp):
        cp.start()
        sent.append(cp)

    def rows(ref, half):
        return ref.at[pl.ds(half * HALF, HALF), :]

    def ag_own(direction, half):
        dst = hbuf.at[1 if direction == 0 else 2]
        return remote(
            rows(h.at[0], half), rows(dst, half),
            ag_s.at[direction, half], ag_r.at[1 + direction, half],
            right if direction == 0 else left,
        )

    def ag_fwd(direction):
        half = direction
        return remote(
            rows(hbuf.at[1 + direction], half), rows(hbuf.at[3], half),
            ag_s.at[direction, 2], ag_r.at[3, half],
            right if direction == 0 else left,
        )

    def ag_wait(slot, half):
        remote(
            rows(hbuf.at[slot], half), rows(hbuf.at[slot], half),
            ag_s.at[0, 0], ag_r.at[slot, half], right,
        ).wait_recv()

    go(ag_own(0, 0))
    go(ag_own(1, 1))
    go(ag_own(0, 1))
    go(ag_own(1, 0))

    QR = D // 4 // NQ

    def region(m, g, core, q, i):
        r = pl.ds(pl.multiple_of(q * (D // 4) + i * QR, QR), QR)
        if m == 0:
            return wq_v.at[g, core, r, :]
        if m == 1:
            return wkv_v.at[g, r, pl.ds(pl.multiple_of(core * HD, HD), HD)]
        return wo_v.at[
            pl.ds(pl.multiple_of((g * 2 + core) * 256, 256), 256),
            pl.ds(pl.multiple_of(i * CW + q * 256, 256), 256),
        ]

    def own_region(m, q, i):
        r = pl.ds(pl.multiple_of(q * (D // 4) + i * QR, QR), QR)
        if m == 0:
            return wq.at[r, :]
        if m == 1:
            return wkv.at[r, :]
        return wo.at[:, pl.ds(pl.multiple_of(i * CW + q * 256, 256), 256)]

    def parts(s):
        return [(0, s), (1, s)] if s < NQ else [(2, s - NQ)]

    def sem_ix(m, i):
        return m * NQ + i

    q_cc = 2 * xl + b
    q_x = 2 * (1 - xl) + b
    q_zc = 2 * xl + 1 - b
    q_zx = 2 * (1 - xl) + 1 - b

    def cross_send(s):
        for m, i in parts(s):
            k = sem_ix(m, i)
            go(remote(own_region(m, q_x, i), region(m, 1, c, q_x, i),
                      w_s.at[0, k], w_r.at[0, k], cross))

    def w_wait(ch, m, core, q, i):
        k = sem_ix(m, i)
        reg = region(m, 1, core, q, i)
        remote(reg, reg, w_s.at[ch, k], w_r.at[ch, k], part).wait_recv()

    def w_send(ch, m, q, i, dev):
        k = sem_ix(m, i)
        reg = region(m, 1, c, q, i)
        go(remote(reg, reg, w_s.at[ch, k], w_r.at[ch, k], dev))

    def ev_cross(s):
        z_dev = zp if s % 2 == 0 else zm
        for m, i in parts(s):
            w_wait(0, m, c, q_cc, i)
            w_send(1, m, q_cc, i, xlo)
            w_send(2, m, q_cc, i, z_dev)
            w_send(4, m, q_cc, i, part)

    def ev_xlo(s):
        z_dev = zp if s % 2 == 0 else zm
        for m, i in parts(s):
            w_wait(1, m, c, q_x, i)
            w_send(3, m, q_x, i, z_dev)
            w_send(5, m, q_x, i, part)

    def ev_zc(s):
        for m, i in parts(s):
            w_wait(2, m, c, q_zc, i)
            w_send(6, m, q_zc, i, part)

    def ev_zx(s):
        for m, i in parts(s):
            w_wait(3, m, c, q_zx, i)
            w_send(7, m, q_zx, i, part)

    def part_wait(steps):
        for s in steps:
            for m, i in parts(s):
                for ch, q in ((4, q_cc), (5, q_x), (6, q_zc), (7, q_zx)):
                    w_wait(ch, m, 1 - c, q, i)

    def own_dst(m, core):
        return (
            wq_v.at[0, core],
            wkv_v.at[0, :, pl.ds(pl.multiple_of(core * HD, HD), HD)],
            wo_v.at[pl.ds(pl.multiple_of(core * 256, 256), 256), :],
        )[m]

    def own_to_part(m):
        go(remote((wq, wkv, wo)[m], own_dst(m, c), po_s.at[m], po_r.at[m], part))

    def own_part_wait(m):
        dst = own_dst(m, 1 - c)
        remote(dst, dst, po_s.at[m], po_r.at[m], part).wait_recv()

    def norm(slot, half):
        @pl.loop(0, HALF // 16)
        def _(r):
            r0 = pl.multiple_of(half * HALF + r * 16, 16)
            wide = hbuf[slot, pl.ds(r0, 16), :].astype(F32)
            ms = jnp.mean(wide * wide, axis=-1, keepdims=True)
            xn[slot, pl.ds(r0, 16), :] = (
                wide * lax.rsqrt(ms + EPS) * gain_v[...]
            ).astype(BF)

    def rope(v):
        return v * tab_v[0] + pltpu.roll(v, HD // 2, 1) * tab_v[1]

    def attn(slot, g):
        x = xn[slot]
        kv = jnp.dot(x, wkv_v[g], preferred_element_type=F32).astype(BF)
        q0 = jnp.dot(x, wq_v[g, 0], preferred_element_type=F32)
        q1 = jnp.dot(x, wq_v[g, 1], preferred_element_type=F32)
        keys = rope(kv[:, :HD].astype(F32)).astype(BF)
        vals = kv[:, HD:]
        qs = jnp.concatenate(
            [rope(v).astype(BF) for v in (q0[:, :HD], q0[:, HD:], q1[:, :HD], q1[:, HD:])],
            axis=0,
        )
        sc = lax.dot_general(
            qs, keys, (((1,), (1,)), ((), ())), preferred_element_type=F32
        ) * (1.0 / math.sqrt(HD))
        rowi = lax.broadcasted_iota(jnp.int32, sc.shape, 0) % SEQ
        coli = lax.broadcasted_iota(jnp.int32, sc.shape, 1)
        sc = jnp.where(rowi >= coli, sc, -1e30)
        e = jnp.exp(sc - jnp.max(sc, axis=-1, keepdims=True))
        p = (e / jnp.sum(e, axis=-1, keepdims=True)).astype(BF)
        o = jnp.dot(p, vals, preferred_element_type=F32).astype(BF)
        for j in range(4):
            mx[slot, :, pl.ds(g * 512 + j * HD, HD)] = o[j * SEQ:(j + 1) * SEQ]

    def outp(slot, i):
        cols = pl.ds(i * CW, CW)
        o = jnp.dot(mx[slot], wo_v[:, cols], preferred_element_type=F32)
        if slot == 0:
            acc[:, cols] = o
        elif slot == 1:
            sbuf[0, pl.ds(0, HALF), cols] = o[:HALF].astype(BF)
            comb[1, :, cols] = o[HALF:]
        elif slot == 2:
            sbuf[1, pl.ds(HALF, HALF), cols] = o[HALF:].astype(BF)
            comb[0, :, cols] = o[:HALF]
        else:
            sbuf[2, :, cols] = o.astype(BF)

    def blk(ref, half, i):
        return ref.at[pl.ds(half * HALF, HALF), pl.ds(i * CW, CW)]

    def y_copy(direction, k, src, dst):
        return remote(src, dst, rs_s.at[direction, k], rs_r.at[direction, k],
                      right if direction == 0 else left)

    def rs_only(d, i):
        return y_copy(d, i, blk(sbuf.at[1 - d], 1 - d, i), blk(rf.at[d], 1 - d, i))

    def rs_diag(d, i):
        return y_copy(d, NC + i, blk(sbuf.at[2], d, i), blk(rd.at[d], 0, i))

    def rs_comb(d, i):
        return y_copy(d, 2 * NC + i, blk(sbuf.at[1 - d], d, i), blk(rf.at[d], d, i))

    def combine(d, i):
        rs_diag(d, i).wait_recv()
        cols = pl.ds(i * CW, CW)
        v = comb[d, :, cols] + rd[d, :, cols].astype(F32)
        sbuf[1 - d, pl.ds(d * HALF, HALF), cols] = v.astype(BF)
        go(rs_comb(d, i))

    outs = []

    def finish(half, i):
        rs_only(1 - half, i).wait_recv()
        rs_comb(half, i).wait_recv()
        rr, cols = pl.ds(half * HALF, HALF), pl.ds(i * CW, CW)
        v = acc[rr, cols] + rf[0, rr, cols].astype(F32) + rf[1, rr, cols].astype(F32)
        ob[rr, cols] = v.astype(BF)
        cp = pltpu.make_async_copy(
            ob.at[rr, cols], out.at[0, rr, cols], sem_o.at[half, i]
        )
        cp.start()
        outs.append(cp)

    plan = []

    def due(time, fn, *args):
        plan.append((time, len(plan), fn, args))

    def loaded(*ks):
        for k in ks:
            loads[k].wait()

    def ag_first():
        ag_wait(1, 0)
        go(ag_fwd(0))
        ag_wait(2, 1)
        go(ag_fwd(1))

    def outp_send(i):
        part_wait([NQ + i])
        outp(2, i)
        go(rs_only(0, i))
        outp(1, i)
        go(rs_only(1, i))

    def outp_diag(i):
        outp(3, i)
        go(rs_diag(0, i))
        go(rs_diag(1, i))

    for s in range(NSTEP):
        tc = 7 + 2.1 * (s + 1) if s < NQ else 7 + 2.1 * NQ + 2.8 * (s - NQ + 1)
        due(tc, ev_cross, s)
        due(tc + 4.1, ev_xlo, s)
        due(tc + 4.1, ev_zc, s)
        due(tc + 8.2, ev_zx, s)
    due(4.5, loaded, 0, 1)
    due(4.5, norm, 0, 0)
    due(4.5, norm, 0, 1)
    due(11.3, loaded, 2, 3, 4)
    due(11.3, own_part_wait, 0)
    due(11.3, own_part_wait, 1)
    due(11.3, attn, 0, 0)
    due(11.4, own_to_part, 2)
    due(18, ag_first)
    due(18, norm, 1, 0)
    due(18, norm, 2, 1)
    due(29.5, ag_wait, 1, 1)
    due(29.5, norm, 1, 1)
    due(29.5, ag_wait, 2, 0)
    due(29.5, norm, 2, 0)
    due(30.5, attn, 2, 0)
    due(32.1, attn, 1, 0)
    due(33.9, part_wait, range(NQ))
    due(33.9, attn, 2, 1)
    due(35.5, attn, 1, 1)
    due(37, loaded, 5)
    due(37, own_part_wait, 2)
    due(37.2, outp_send, 0)
    due(38.5, attn, 0, 1)
    due(40.3, outp_send, 1)
    due(40.8, ag_wait, 3, 0)
    due(40.8, ag_wait, 3, 1)
    due(40.8, norm, 3, 0)
    due(40.8, norm, 3, 1)
    due(42, attn, 3, 0)
    due(43.3, outp_send, 2)
    due(44, attn, 3, 1)
    due(46, outp_send, 3)
    for i in range(NC):
        due(47, outp_diag, i)
    for i in range(NC):
        due(48, outp, 0, i)
    for i in range(NC):
        due(50, combine, 0, i)
        due(50, combine, 1, i)
    for i in range(NC):
        due(60, finish, 0, i)
        due(60, finish, 1, i)

    for s in range(NSTEP):
        cross_send(s)
    own_to_part(0)
    own_to_part(1)
    for time, _, fn, args in sorted(plan, key=lambda p: p[:2]):
        fn(*args)
    for cp in outs:
        cp.wait()
    for cp in sent:
        cp.wait_send()


def shards(hidden_in, norm_gain, query_weight, kv_weight, output_weight):
    tab = jnp.asarray(tables())
    anyspec = pl.BlockSpec(memory_space=pl.ANY)
    dma = pltpu.SemaphoreType.DMA
    return pl.pallas_call(
        kernel,
        out_shape=jax.ShapeDtypeStruct((1, SEQ, D), BF),
        in_specs=[anyspec] * 6,
        out_specs=anyspec,
        scratch_shapes=[
            pltpu.VMEM((4, SEQ, D), BF),
            pltpu.VMEM((4, SEQ, D), BF),
            pltpu.VMEM((1, D), F32),
            pltpu.VMEM((2, SEQ, HD), F32),
            pltpu.VMEM((2, 2, D, 2 * HD), BF),
            pltpu.VMEM((2, D, 2 * HD), BF),
            pltpu.VMEM((1024, D), BF),
            pltpu.VMEM((4, SEQ, 1024), BF),
            pltpu.VMEM((SEQ, D), F32),
            pltpu.VMEM((2, HALF, D), F32),
            pltpu.VMEM((3, SEQ, D), BF),
            pltpu.VMEM((2, HALF, D), BF),
            pltpu.VMEM((2, SEQ, D), BF),
            pltpu.VMEM((SEQ, D), BF),
            dma((6,)),
            dma((2, NC)),
            dma((2, 3)),
            dma((4, 2)),
            dma((8, 2 * NQ + NC)),
            dma((8, 2 * NQ + NC)),
            dma((3,)),
            dma((3,)),
            dma((2, 3 * NC)),
            dma((2, 3 * NC)),
        ],
        compiler_params=pltpu.CompilerParams(
            collective_id=0, has_side_effects=True, vmem_limit_bytes=67000000
        ),
        cost_estimate=pl.CostEstimate(
            flops=11_000_000_000, bytes_accessed=8_000_000, transcendentals=600_000
        ),
    )(hidden_in, norm_gain.reshape(1, D), tab, query_weight, kv_weight, output_weight)


def solution(mesh):
    placed = (
        P(("dp", "tensor"), None, None),
        P(),
        P(None, "tensor"),
        P(None, "tensor"),
        P("tensor", None),
    )
    return jax.shard_map(
        shards,
        mesh=mesh,
        in_specs=placed,
        out_specs=P(("dp", "tensor"), None, None),
        check_vma=False,
    )
```

time: 102 us -> 91.3 us (0.90); the launches traced: 102 us -> 90.1 us
  Pallas kernels: 99.6 us -> 87.8 us
    pallas_call x1, Pallas kernels: 99.6 us -> 87.8 us  [shards(): pl.pallas_call(kernel, out_shape=jax.ShapeDtypeStruct((1, SEQ, D), BF), i...]
where the time goes in v2:
time: 91.3 us; the launch traced here: 90.1 us
  Pallas kernels  87.8 us (96%)
  local copies, waits for them, and re-layouts  2.29 us (3%)
    pallas_call x1, Pallas kernels, shards(): pl.pallas_call(kernel, out_shape=jax.ShapeDtypeStruct((1, SEQ, D), BF), i...  87.8 us
    unnamed x1, local copies, waits for them, and re-layouts  2.29 us

profile of v2, /device:TPU:1, one launch (start us, length us, event | category | flops | bytes accessed | tf_op | source)
XLA Modules:
  0.0 90.1 jit_solution(15907697378903413322)
XLA Ops:
  0.0 87.8 %shard_map.64 = bf16[1,128,4096]{2,1,0:T(8,128)(2,1)} custom-call(bf16[1,128,4096]{2,1,0:T(8,128)(2,1)} %h.1, f32[1,4096]{1,0:T(1,128)} %bitcast.1, f32[2,128,128]{2,1,0:T(8,128)} %constant.2.clone.tab, bf16[4096,256]{1,0:T(8,128)(2,1)} %wq.1, bf16[4096,128]{1,0:T(8,128)(2,1)} %wkv.1, bf16[256,4096]{1,0:T(8,128)(2,1)} %wo.1), custom_call_target="tpu_custom_call" | custom-call | flops 11000000512 | bytes 8000000 | tf_op jit(solution)/shard_map/pallas_call | solution.py:392
  87.8 2.3 %copy.8 = bf16[1,128,4096]{2,1,0:T(8,128)(2,1)} copy(bf16[1,128,4096]{2,1,0:T(8,128)(2,1)} %shard_map.64) | data formatting | bytes 2097152

commit v3 on v2

--- a/solution.py
+++ b/solution.py
@@ -14,10 +14,16 @@
 SEQ = 128
 D = 4096
 HALF = SEQ // 2
-CW = 1024
-NC = D // CW
-NQ = 8
+QROWS = (80, 80, 96, 128, 128, 96, 80, 80, 96, 96, 64)
+QOFF = tuple(sum(QROWS[:i]) for i in range(len(QROWS)))
+NQ = len(QROWS)
+GROUPS = ((0, 5, 0, 512), (5, 3, 512, 256), (8, 3, 768, 256))
+CWS = (512, 512, 1024, 1024, 512, 512)
+COFF = tuple(sum(CWS[:i]) for i in range(len(CWS)))
+NC = len(CWS)
 NSTEP = NQ + NC
+DIRECT = NQ + 2
+QD = D // 4
 BF = jnp.bfloat16
 F32 = jnp.float32
 MESH = pl.DeviceIdType.MESH
@@ -32,9 +38,35 @@
     ).astype(np.float32)
 
 
+def arrivals(start):
+    rate, hop = 46.6e3, 2.0
+    size = [2 * r * 3 * HD for r in QROWS] + [2 * 2 * HD * w // 4 for w in CWS]
+    wire = [b / rate for b in size]
+    t_zc, t_zx = [0.0] * NSTEP, [0.0] * NSTEP
+    t_c, free = [], start + 1.0
+    for w in wire:
+        free += w
+        t_c.append(free + hop)
+    for s in range(DIRECT, NSTEP):
+        free += wire[s]
+        t_zx[s] = free + hop
+    t_x, free = [], 0.0
+    for s, w in enumerate(wire):
+        free = max(free, t_c[s]) + w
+        t_x.append(free + hop)
+    for side in (0, 1):
+        jobs = [(t_c[s], 0, s) for s in range(side, NSTEP, 2)]
+        jobs += [(t_x[s], 1, s) for s in range(side, DIRECT, 2)]
+        free = 0.0
+        for ready, kind, s in sorted(jobs):
+            free = max(free, ready) + wire[s]
+            (t_zc, t_zx)[kind][s] = free + hop
+    return t_c, t_x, t_zc, t_zx
+
+
 def kernel(
     h, gain, tab, wq, wkv, wo, out,
-    hbuf, xn, gain_v, tab_v, wq_v, wkv_v, wo_v, mx,
+    hbuf, xn, gain_v, tab_v, wq_v, wkv_v, wo_v, mx, pacc,
     acc, comb, sbuf, rd, rf, ob,
     sem_l, sem_o, ag_s, ag_r, w_s, w_r, po_s, po_r, rs_s, rs_r,
 ):
@@ -116,26 +148,30 @@
     go(ag_own(0, 1))
     go(ag_own(1, 0))
 
-    QR = D // 4 // NQ
+    def qrows(q, i):
+        return pl.ds(pl.multiple_of(q * QD + QOFF[i], 16), QROWS[i])
+
+    def qcols(q, i):
+        w = CWS[i] // 4
+        return pl.ds(pl.multiple_of(COFF[i] + q * w, w), w)
 
     def region(m, g, core, q, i):
-        r = pl.ds(pl.multiple_of(q * (D // 4) + i * QR, QR), QR)
+        r = qrows(q, i) if m < 2 else None
         if m == 0:
             return wq_v.at[g, core, r, :]
         if m == 1:
             return wkv_v.at[g, r, pl.ds(pl.multiple_of(core * HD, HD), HD)]
         return wo_v.at[
             pl.ds(pl.multiple_of((g * 2 + core) * 256, 256), 256),
-            pl.ds(pl.multiple_of(i * CW + q * 256, 256), 256),
+            qcols(q, i),
         ]
 
     def own_region(m, q, i):
-        r = pl.ds(pl.multiple_of(q * (D // 4) + i * QR, QR), QR)
         if m == 0:
-            return wq.at[r, :]
+            return wq.at[qrows(q, i), :]
         if m == 1:
-            return wkv.at[r, :]
-        return wo.at[:, pl.ds(pl.multiple_of(i * CW + q * 256, 256), 256)]
+            return wkv.at[qrows(q, i), :]
+        return wo.at[:, qcols(q, i)]
 
     def parts(s):
         return [(0, s), (1, s)] if s < NQ else [(2, s - NQ)]
@@ -154,6 +190,12 @@
             go(remote(own_region(m, q_x, i), region(m, 1, c, q_x, i),
                       w_s.at[0, k], w_r.at[0, k], cross))
 
+    def across_send(s):
+        for m, i in parts(s):
+            k = sem_ix(m, i)
+            go(remote(own_region(m, q_zc, i), region(m, 1, c, q_zc, i),
+                      w_s.at[3, k], w_r.at[3, k], cross))
+
     def w_wait(ch, m, core, q, i):
         k = sem_ix(m, i)
         reg = region(m, 1, core, q, i)
@@ -165,7 +207,7 @@
         go(remote(reg, reg, w_s.at[ch, k], w_r.at[ch, k], dev))
 
     def ev_cross(s):
-        z_dev = zp if s % 2 == 0 else zm
+        z_dev = (zp, zm)[s % 2]
         for m, i in parts(s):
             w_wait(0, m, c, q_cc, i)
             w_send(1, m, q_cc, i, xlo)
@@ -173,10 +215,11 @@
             w_send(4, m, q_cc, i, part)
 
     def ev_xlo(s):
-        z_dev = zp if s % 2 == 0 else zm
+        z_dev = (zp, zm)[s % 2]
         for m, i in parts(s):
             w_wait(1, m, c, q_x, i)
-            w_send(3, m, q_x, i, z_dev)
+            if s < DIRECT:
+                w_send(3, m, q_x, i, z_dev)
             w_send(5, m, q_x, i, part)
 
     def ev_zc(s):
@@ -215,18 +258,14 @@
             r0 = pl.multiple_of(half * HALF + r * 16, 16)
             wide = hbuf[slot, pl.ds(r0, 16), :].astype(F32)
             ms = jnp.mean(wide * wide, axis=-1, keepdims=True)
-            xn[slot, pl.ds(r0, 16), :] = (
+            xn[pl.ds(pl.multiple_of(slot * SEQ + r0, 16), 16), :] = (
                 wide * lax.rsqrt(ms + EPS) * gain_v[...]
             ).astype(BF)
 
     def rope(v):
         return v * tab_v[0] + pltpu.roll(v, HD // 2, 1) * tab_v[1]
 
-    def attn(slot, g):
-        x = xn[slot]
-        kv = jnp.dot(x, wkv_v[g], preferred_element_type=F32).astype(BF)
-        q0 = jnp.dot(x, wq_v[g, 0], preferred_element_type=F32)
-        q1 = jnp.dot(x, wq_v[g, 1], preferred_element_type=F32)
+    def attend(slot, g, kv, q0, q1):
         keys = rope(kv[:, :HD].astype(F32)).astype(BF)
         vals = kv[:, HD:]
         qs = jnp.concatenate(
@@ -245,8 +284,69 @@
         for j in range(4):
             mx[slot, :, pl.ds(g * 512 + j * HD, HD)] = o[j * SEQ:(j + 1) * SEQ]
 
+    def project(x, g, ks):
+        def chain(w, some):
+            v = None
+            for k0, kn in some:
+                d = jnp.dot(x(k0, kn), w[pl.ds(k0, kn), :], preferred_element_type=F32)
+                v = d if v is None else v + d
+            return v
+
+        h = len(ks) // 2
+        q0 = chain(wq_v.at[g, 0], ks)
+        q1 = chain(wq_v.at[g, 1], ks)
+        kv = chain(wkv_v.at[g], ks[:h]) + chain(wkv_v.at[g], ks[h:])
+        return kv, q0, q1
+
+    ALL_K = [(0, D // 2), (D // 2, D // 2)]
+
+    def group_k(j):
+        _, _, k0, kn = GROUPS[j]
+        return [(q * QD + k0, kn) for q in range(4)]
+
+    def attn(slot, g):
+        kv, q0, q1 = project(
+            lambda k0, kn: xn[pl.ds(slot * SEQ, SEQ), pl.ds(k0, kn)], g, ALL_K
+        )
+        attend(slot, g, kv.astype(BF), q0, q1)
+
+    SETS = (((1, 0), (2, 1)), ((1, 1), (2, 0)))
+
+    def proj_set(n, g, j):
+        def x(k0, kn):
+            return jnp.concatenate(
+                [xn[pl.ds(sl * SEQ + hf * HALF, HALF), pl.ds(k0, kn)] for sl, hf in SETS[n]],
+                axis=0,
+            )
+
+        for m, v in enumerate(project(x, g, ALL_K if j is None else group_k(j))):
+            for u, (sl, hf) in enumerate(SETS[n]):
+                pacc[g, m, pl.ds((sl - 1) * SEQ + hf * HALF, HALF), :] = v[
+                    u * HALF:(u + 1) * HALF
+                ]
+
+    def proj_both(g, j):
+        vs = project(
+            lambda k0, kn: xn[pl.ds(SEQ, 2 * SEQ), pl.ds(k0, kn)], g, group_k(j)
+        )
+        vs = [pacc[g, m] + v for m, v in enumerate(vs)]
+        if j < 2:
+            for m, v in enumerate(vs):
+                pacc[g, m] = v
+        else:
+            attend_both(g, vs)
+
+    def attend_both(g, vs=None):
+        for u in (1, 0):
+            r = pl.ds(u * SEQ, SEQ)
+            kv, q0, q1 = [
+                pacc[g, m, r] if vs is None else vs[m][u * SEQ:(u + 1) * SEQ]
+                for m in range(3)
+            ]
+            attend(1 + u, g, kv.astype(BF), q0, q1)
+
     def outp(slot, i):
-        cols = pl.ds(i * CW, CW)
+        cols = pl.ds(COFF[i], CWS[i])
         o = jnp.dot(mx[slot], wo_v[:, cols], preferred_element_type=F32)
         if slot == 0:
             acc[:, cols] = o
@@ -260,7 +360,7 @@
             sbuf[2, :, cols] = o.astype(BF)
 
     def blk(ref, half, i):
-        return ref.at[pl.ds(half * HALF, HALF), pl.ds(i * CW, CW)]
+        return ref.at[pl.ds(half * HALF, HALF), pl.ds(COFF[i], CWS[i])]
 
     def y_copy(direction, k, src, dst):
         return remote(src, dst, rs_s.at[direction, k], rs_r.at[direction, k],
@@ -277,7 +377,7 @@
 
     def combine(d, i):
         rs_diag(d, i).wait_recv()
-        cols = pl.ds(i * CW, CW)
+        cols = pl.ds(COFF[i], CWS[i])
         v = comb[d, :, cols] + rd[d, :, cols].astype(F32)
         sbuf[1 - d, pl.ds(d * HALF, HALF), cols] = v.astype(BF)
         go(rs_comb(d, i))
@@ -287,7 +387,7 @@
     def finish(half, i):
         rs_only(1 - half, i).wait_recv()
         rs_comb(half, i).wait_recv()
-        rr, cols = pl.ds(half * HALF, HALF), pl.ds(i * CW, CW)
+        rr, cols = pl.ds(half * HALF, HALF), pl.ds(COFF[i], CWS[i])
         v = acc[rr, cols] + rf[0, rr, cols].astype(F32) + rf[1, rr, cols].astype(F32)
         ob[rr, cols] = v.astype(BF)
         cp = pltpu.make_async_copy(
@@ -323,12 +423,16 @@
         go(rs_diag(0, i))
         go(rs_diag(1, i))
 
+    t_c, t_x, t_zc, t_zx = arrivals(5.0)
+    landed = [max(ts) + 2 for ts in zip(t_c, t_x, t_zc, t_zx)]
+    last_qkv = max(landed[:NQ])
+    written = []
     for s in range(NSTEP):
-        tc = 7 + 2.1 * (s + 1) if s < NQ else 7 + 2.1 * NQ + 2.8 * (s - NQ + 1)
-        due(tc, ev_cross, s)
-        due(tc + 4.1, ev_xlo, s)
-        due(tc + 4.1, ev_zc, s)
-        due(tc + 8.2, ev_zx, s)
+        for time, ev in ((t_c, ev_cross), (t_x, ev_xlo), (t_zc, ev_zc), (t_zx, ev_zx)):
+            if time[s] < last_qkv:
+                due(time[s], ev, s)
+            else:
+                written.append((ev, s))
     due(4.5, loaded, 0, 1)
     due(4.5, norm, 0, 0)
     due(4.5, norm, 0, 1)
@@ -337,47 +441,88 @@
     due(11.3, own_part_wait, 1)
     due(11.3, attn, 0, 0)
     due(11.4, own_to_part, 2)
-    due(18, ag_first)
-    due(18, norm, 1, 0)
-    due(18, norm, 2, 1)
-    due(29.5, ag_wait, 1, 1)
-    due(29.5, norm, 1, 1)
-    due(29.5, ag_wait, 2, 0)
-    due(29.5, norm, 2, 0)
-    due(30.5, attn, 2, 0)
-    due(32.1, attn, 1, 0)
-    due(33.9, part_wait, range(NQ))
-    due(33.9, attn, 2, 1)
-    due(35.5, attn, 1, 1)
-    due(37, loaded, 5)
-    due(37, own_part_wait, 2)
-    due(37.2, outp_send, 0)
-    due(38.5, attn, 0, 1)
-    due(40.3, outp_send, 1)
-    due(40.8, ag_wait, 3, 0)
-    due(40.8, ag_wait, 3, 1)
-    due(40.8, norm, 3, 0)
-    due(40.8, norm, 3, 1)
-    due(42, attn, 3, 0)
-    due(43.3, outp_send, 2)
-    due(44, attn, 3, 1)
-    due(46, outp_send, 3)
+    due(18.5, ag_first)
+    due(18.5, norm, 1, 0)
+    due(18.5, norm, 2, 1)
+    due(19.5, proj_set, 0, 0, None)
+    due(30, ag_wait, 1, 1)
+    due(30, norm, 1, 1)
+    due(30, ag_wait, 2, 0)
+    due(30, norm, 2, 0)
+    due(30.5, proj_set, 1, 0, None)
+    for j, (i0, n, _, _) in enumerate(GROUPS):
+        when = max(landed[i0:i0 + n])
+        if j == 2:
+            due(when, attend_both, 0)
+        due(when, part_wait, range(i0, i0 + n))
+        if j == 0:
+            due(when, proj_set, 0, 1, 0)
+            due(max(when, 31.5), proj_set, 1, 1, 0)
+        else:
+            due(max(when, 32.6), proj_both, 1, j)
+
+    def then(fn, *args):
+        due(last_qkv + 1, fn, *args)
+
+    def relays(upto):
+        for ev in (ev_cross, ev_xlo, ev_zc, ev_zx):
+            for w in [w for w in written if w[0] is ev and w[1] <= NQ + upto]:
+                then(*w)
+                written.remove(w)
+
+    then(loaded, 5)
+    then(own_part_wait, 2)
+    relays(0)
+    then(outp_send, 0)
+    for w in [w for w in written if w[0] is ev_cross]:
+        then(*w)
+        written.remove(w)
+    relays(2)
+    then(attn, 0, 1)
+    then(outp_send, 1)
+    then(outp_send, 2)
+    relays(3)
+    for half in (0, 1):
+        then(ag_wait, 3, half)
+        then(norm, 3, half)
+    then(outp_send, 3)
+    relays(5)
+    then(attn, 3, 0)
+    then(outp_send, 4)
+    then(outp_send, 5)
+    then(attn, 3, 1)
     for i in range(NC):
-        due(47, outp_diag, i)
+        then(outp_diag, i)
     for i in range(NC):
-        due(48, outp, 0, i)
+        then(outp, 0, i)
     for i in range(NC):
-        due(50, combine, 0, i)
-        due(50, combine, 1, i)
+        then(combine, 0, i)
+        then(combine, 1, i)
     for i in range(NC):
-        due(60, finish, 0, i)
-        due(60, finish, 1, i)
-
+        then(finish, 0, i)
+        then(finish, 1, i)
+
+    assert not written
     for s in range(NSTEP):
         cross_send(s)
+    for s in range(DIRECT, NSTEP):
+        across_send(s)
     own_to_part(0)
     own_to_part(1)
-    for time, _, fn, args in sorted(plan, key=lambda p: p[:2]):
+    plan.sort(key=lambda p: p[:2])
+    at = {(p[2], p[3]): k for k, p in enumerate(plan)}
+    for i in range(NC):
+        assert at[outp_send, (i,)] > max(at[ev_zx, (NQ + i,)], at[ev_zc, (NQ + i,)])
+        assert at[outp_diag, (i,)] > at[outp_send, (i,)]
+    for s in range(NSTEP):
+        assert at[ev_cross, (s,)] < at[ev_xlo, (s,)] < at[ev_zx, (s,)]
+        assert at[ev_cross, (s,)] < at[ev_zc, (s,)]
+    for j, (i0, n, _, _) in enumerate(GROUPS):
+        for s in range(i0, i0 + n):
+            pj = (proj_both, (1, j)) if j else (proj_set, (0, 1, 0))
+            assert at[pj] > max(at[ev_zx, (s,)], at[ev_zc, (s,)])
+            assert at[part_wait, (range(i0, i0 + n),)] > max(at[ev_zx, (s,)], at[ev_zc, (s,)])
+    for time, _, fn, args in plan:
         fn(*args)
     for cp in outs:
         cp.wait()
@@ -396,13 +541,14 @@
         out_specs=anyspec,
         scratch_shapes=[
             pltpu.VMEM((4, SEQ, D), BF),
-            pltpu.VMEM((4, SEQ, D), BF),
+            pltpu.VMEM((4 * SEQ, D), BF),
             pltpu.VMEM((1, D), F32),
             pltpu.VMEM((2, SEQ, HD), F32),
             pltpu.VMEM((2, 2, D, 2 * HD), BF),
             pltpu.VMEM((2, D, 2 * HD), BF),
             pltpu.VMEM((1024, D), BF),
             pltpu.VMEM((4, SEQ, 1024), BF),
+            pltpu.VMEM((2, 3, 2 * SEQ, 2 * HD), F32),
             pltpu.VMEM((SEQ, D), F32),
             pltpu.VMEM((2, HALF, D), F32),
             pltpu.VMEM((3, SEQ, D), BF),

time: 91.3 us -> 88.3 us (0.967); the launches traced: 90.1 us -> 88.2 us
  Pallas kernels: 87.8 us -> 85.9 us
    pallas_call x1, Pallas kernels: 87.8 us -> 85.9 us  [shards(): pl.pallas_call(kernel, out_shape=jax.ShapeDtypeStruct((1, SEQ, D), BF), i...]
where the time goes in v3:
time: 88.3 us; the launch traced here: 88.2 us
  Pallas kernels  85.9 us (97%)
  local copies, waits for them, and re-layouts  2.29 us (3%)
    pallas_call x1, Pallas kernels, shards(): pl.pallas_call(kernel, out_shape=jax.ShapeDtypeStruct((1, SEQ, D), BF), i...  85.9 us
    unnamed x1, local copies, waits for them, and re-layouts  2.29 us

profile of v3, /device:TPU:1, one launch (start us, length us, event | category | flops | bytes accessed | tf_op | source)
XLA Modules:
  0.0 88.2 jit_solution(12176971982487043206)
XLA Ops:
  0.0 85.9 %shard_map.64 = bf16[1,128,4096]{2,1,0:T(8,128)(2,1)} custom-call(bf16[1,128,4096]{2,1,0:T(8,128)(2,1)} %h.1, f32[1,4096]{1,0:T(1,128)} %bitcast.1, f32[2,128,128]{2,1,0:T(8,128)} %constant.2.clone.tab, bf16[4096,256]{1,0:T(8,128)(2,1)} %wq.1, bf16[4096,128]{1,0:T(8,128)(2,1)} %wkv.1, bf16[256,4096]{1,0:T(8,128)(2,1)} %wo.1), custom_call_target="tpu_custom_call" | custom-call | flops 11000000512 | bytes 8000000 | tf_op jit(solution)/shard_map/pallas_call | solution.py:537
  85.9 2.3 %copy.8 = bf16[1,128,4096]{2,1,0:T(8,128)(2,1)} copy(bf16[1,128,4096]{2,1,0:T(8,128)(2,1)} %shard_map.64) | data formatting | bytes 2097152

commit v4 on v3

--- a/solution.py
+++ b/solution.py
@@ -68,7 +68,7 @@
     h, gain, tab, wq, wkv, wo, out,
     hbuf, xn, gain_v, tab_v, wq_v, wkv_v, wo_v, mx, pacc,
     acc, comb, sbuf, rd, rf, ob,
-    sem_l, sem_o, ag_s, ag_r, w_s, w_r, po_s, po_r, rs_s, rs_r,
+    sem_l, sem_o, ag_s, ag_r, w_s, w_r, p_r, po_s, po_r, rs_s, rs_r,
 ):
     dp = lax.axis_index("dp")
     t = lax.axis_index("tensor")
@@ -187,24 +187,29 @@
     def cross_send(s):
         for m, i in parts(s):
             k = sem_ix(m, i)
-            go(remote(own_region(m, q_x, i), region(m, 1, c, q_x, i),
-                      w_s.at[0, k], w_r.at[0, k], cross))
+            remote(own_region(m, q_x, i), region(m, 1, c, q_x, i),
+                   w_s.at[0, m], w_r.at[0, k], cross).start()
 
     def across_send(s):
         for m, i in parts(s):
             k = sem_ix(m, i)
-            go(remote(own_region(m, q_zc, i), region(m, 1, c, q_zc, i),
-                      w_s.at[3, k], w_r.at[3, k], cross))
+            remote(own_region(m, q_zc, i), region(m, 1, c, q_zc, i),
+                   w_s.at[3, m], w_r.at[3, k], cross).start()
 
     def w_wait(ch, m, core, q, i):
         k = sem_ix(m, i)
         reg = region(m, 1, core, q, i)
-        remote(reg, reg, w_s.at[ch, k], w_r.at[ch, k], part).wait_recv()
+        remote(reg, reg, w_s.at[ch, m], w_r.at[ch, k], part).wait_recv()
 
     def w_send(ch, m, q, i, dev):
-        k = sem_ix(m, i)
         reg = region(m, 1, c, q, i)
-        go(remote(reg, reg, w_s.at[ch, k], w_r.at[ch, k], dev))
+        if ch < 4:
+            got = w_r.at[ch, sem_ix(m, i)]
+        elif m < 2:
+            got = p_r.at[m * 3 + sum(i >= g[0] for g in GROUPS[1:])]
+        else:
+            got = p_r.at[6 + i]
+        remote(reg, reg, w_s.at[min(ch, 4), m], got, dev).start()
 
     def ev_cross(s):
         z_dev = (zp, zm)[s % 2]
@@ -232,11 +237,30 @@
             w_wait(3, m, c, q_zx, i)
             w_send(7, m, q_zx, i, part)
 
+    def some(m, core, rows, cols):
+        if m == 0:
+            return wq_v.at[1, core, pl.ds(0, rows), :]
+        if m == 1:
+            return wkv_v.at[1, pl.ds(0, rows), pl.ds(pl.multiple_of(core * HD, HD), HD)]
+        return wo_v.at[pl.ds(pl.multiple_of((2 + core) * 256, 256), 256), cols]
+
     def part_wait(steps):
-        for s in steps:
-            for m, i in parts(s):
-                for ch, q in ((4, q_cc), (5, q_x), (6, q_zc), (7, q_zx)):
-                    w_wait(ch, m, 1 - c, q, i)
+        s0 = steps[0]
+        for m in (0, 1) if s0 < NQ else (2,):
+            if m < 2:
+                reg = some(m, 1 - c, 4 * sum(QROWS[s] for s in steps), None)
+                got = p_r.at[m * 3 + sum(s0 >= g[0] for g in GROUPS[1:])]
+            else:
+                reg = some(2, 1 - c, None, pl.ds(COFF[s0 - NQ], CWS[s0 - NQ]))
+                got = p_r.at[6 + s0 - NQ]
+            remote(reg, reg, w_s.at[4, m], got, part).wait_recv()
+
+    def weights_sent():
+        for kind in range(5):
+            for m in range(3):
+                n = D if kind == 4 else QD
+                reg = some(m, c, n, pl.ds(0, n))
+                remote(reg, reg, w_s.at[kind, m], w_r.at[0, 0], part).wait_send()
 
     def own_dst(m, core):
         return (
@@ -528,6 +552,7 @@
         cp.wait()
     for cp in sent:
         cp.wait_send()
+    weights_sent()
 
 
 def shards(hidden_in, norm_gain, query_weight, kv_weight, output_weight):
@@ -559,8 +584,9 @@
             dma((2, NC)),
             dma((2, 3)),
             dma((4, 2)),
-            dma((8, 2 * NQ + NC)),
-            dma((8, 2 * NQ + NC)),
+            dma((5, 3)),
+            dma((4, 2 * NQ + NC)),
+            dma((6 + NC,)),
             dma((3,)),
             dma((3,)),
             dma((2, 3 * NC)),

time: 88.3 us -> 85.2 us (0.965)
  Pallas kernels: 85.9 us -> 82.8 us
    pallas_call x1, Pallas kernels: 85.9 us -> 82.8 us  [shards(): pl.pallas_call(kernel, out_shape=jax.ShapeDtypeStruct((1, SEQ, D), BF), i...]
where the time goes in v4:
time: 85.2 us; the launch traced here: 85.1 us
  Pallas kernels  82.8 us (97%)
  local copies, waits for them, and re-layouts  2.29 us (3%)
    pallas_call x1, Pallas kernels, shards(): pl.pallas_call(kernel, out_shape=jax.ShapeDtypeStruct((1, SEQ, D), BF), i...  82.8 us
    unnamed x1, local copies, waits for them, and re-layouts  2.29 us

profile of v4, /device:TPU:1, one launch (start us, length us, event | category | flops | bytes accessed | tf_op | source)
XLA Modules:
  0.0 85.1 jit_solution(11420865974994487757)
XLA Ops:
  0.0 82.8 %shard_map.64 = bf16[1,128,4096]{2,1,0:T(8,128)(2,1)} custom-call(bf16[1,128,4096]{2,1,0:T(8,128)(2,1)} %h.1, f32[1,4096]{1,0:T(1,128)} %bitcast.1, f32[2,128,128]{2,1,0:T(8,128)} %constant.2.clone.tab, bf16[4096,256]{1,0:T(8,128)(2,1)} %wq.1, bf16[4096,128]{1,0:T(8,128)(2,1)} %wkv.1, bf16[256,4096]{1,0:T(8,128)(2,1)} %wo.1), custom_call_target="tpu_custom_call" | custom-call | flops 11000000512 | bytes 8000000 | tf_op jit(solution)/shard_map/pallas_call | solution.py:562
  82.8 2.3 %copy.8 = bf16[1,128,4096]{2,1,0:T(8,128)(2,1)} copy(bf16[1,128,4096]{2,1,0:T(8,128)(2,1)} %shard_map.64) | data formatting | bytes 2097152
